TPU v7x, 32 devices: a whole 2x2x4 slice. The times are simulated.
32 devices in a mesh: row: 4 (over y, core), col: 8 (over z, x).
Axes of the slice: x: 2, y: 2, z: 4, core: 2. Of those that a mesh axis runs over, the one named last changes fastest.
Arguments:
- nodes: bfloat16 [32768, 512], P(('row', 'col')), may hold values from -8 to 8
- ln1_gain: float32 [512], replicated, may hold values from 0.25 to 1.75
- w_qkv: bfloat16 [512, 1536], replicated, may hold values from -1 to 1
- w_out: bfloat16 [512, 512], replicated, may hold values from -0.25 to 0.25
- ln2_gain: float32 [512], replicated, may hold values from 0.25 to 1.75
- w_up: bfloat16 [512, 2048], replicated, may hold values from -0.25 to 0.25
- w_down: bfloat16 [2048, 512], replicated, may hold values from -0.125 to 0.125
- adjacency: int32 [32768, 128], P(('row', 'col')), may hold values 0 or 1
- remote_ids: int32 [32, 10], replicated, may hold values from 0 to 255, as said below
- remote_live: int32 [32, 10], replicated, may hold values from 0 to 1, as said below
Outputs:
- updated: bfloat16 [32768, 512], P(('row', 'col'))
Inputs may be any that keep to these rules, and one draw needn't show every extreme that they name: `remote_ids`: every entry of device d's list names a block of another device in d's row or d's column of the mesh; the entries of one list are distinct; at most 1 live entries of one list name blocks of one device, and some list has exactly 1 from one device. `remote_live`: some device has all 10 entries live; every device has 8 or more.
All inputs are finite; a program needn't handle non-finite values. No bound on the sum of `adjacency` on one device may be relied on, other than what follows from the above.
Results may differ from a plain program's by a relative error of at most 0.005.
Values may be sent and summed in bfloat16 or wider, within the bound.
A program may use at most 128 MiB of HBM per device.

v0:
```python
import math
import jax
import jax.numpy as jnp
from jax import lax
from jax.sharding import PartitionSpec as P

HEADS = 8
BLK = 128
CAP = 1
EPS = 1e-05
NEG_FILL = -1e30


def normalize(values, gain):
    values = values.astype(jnp.float32)
    row_mean = jnp.mean(values, axis=-1, keepdims=True)
    centered = values - row_mean
    row_var = jnp.mean(centered * centered, axis=-1, keepdims=True)
    return (centered * lax.rsqrt(row_var + EPS) * gain).astype(jnp.bfloat16)


def attend(queries, local_kv, remote_kv, adj_rows, key_alive):
    row_count = queries.shape[0]
    model_width = queries.shape[1]
    head_dim = model_width // HEADS
    block_count = row_count // BLK
    score_scale = 1.0 / math.sqrt(head_dim)
    query_h = queries.reshape(block_count, BLK, HEADS, head_dim)
    local_keys = local_kv[:, :model_width].reshape(block_count, BLK, HEADS, head_dim)
    local_vals = local_kv[:, model_width:].reshape(block_count, BLK, HEADS, head_dim)
    remote_keys = remote_kv[:, :model_width].reshape(-1, HEADS, head_dim)
    remote_vals = remote_kv[:, model_width:].reshape(-1, HEADS, head_dim)
    local_scores = (
        jnp.einsum("bihd,bjhd->bhij", query_h, local_keys, preferred_element_type=jnp.float32)
        * score_scale
    )
    eye_mask = jnp.arange(BLK)[:, None] == jnp.arange(BLK)[None, :]
    allowed = (adj_rows.reshape(block_count, BLK, BLK) > 0) | eye_mask[None]
    local_scores = jnp.where(allowed[:, None], local_scores, NEG_FILL)
    remote_scores = (
        jnp.einsum("bihd,jhd->bhij", query_h, remote_keys, preferred_element_type=jnp.float32)
        * score_scale
    )
    remote_scores = jnp.where(key_alive[None, None, None, :] > 0, remote_scores, NEG_FILL)
    row_max = jnp.maximum(jnp.max(local_scores, axis=-1), jnp.max(remote_scores, axis=-1))
    local_exp = jnp.exp(local_scores - row_max[..., None])
    remote_exp = jnp.exp(remote_scores - row_max[..., None])
    row_total = jnp.sum(local_exp, axis=-1) + jnp.sum(remote_exp, axis=-1)
    local_probs = (local_exp / row_total[..., None]).astype(jnp.bfloat16)
    remote_probs = (remote_exp / row_total[..., None]).astype(jnp.bfloat16)
    summed = jnp.einsum(
        "bhij,bjhd->bihd", local_probs, local_vals, preferred_element_type=jnp.float32
    )
    summed = summed + jnp.einsum(
        "bhij,jhd->bihd", remote_probs, remote_vals, preferred_element_type=jnp.float32
    )
    return summed.reshape(row_count, model_width).astype(jnp.bfloat16)


def choose_blocks(owner_rows, rank_rows, alive_rows, local_rows, self_index):
    cap_iota = jnp.arange(CAP, dtype=jnp.int32)
    matched = (
        alive_rows[:, None, :]
        & (owner_rows[:, None, :] == self_index)
        & (rank_rows[:, None, :] == cap_iota[None, :, None])
    )
    return jnp.sum(matched.astype(jnp.int32) * local_rows[:, None, :], axis=2)


def outgoing(source, chosen_local, peer_count):
    picked = jnp.take(source, chosen_local.reshape(-1), axis=0, mode="clip")
    return picked.reshape(peer_count, CAP, BLK, source.shape[2])


def shards(
    nodes, ln1_gain, w_qkv, w_out, ln2_gain, w_up, w_down, adjacency, remote_ids, remote_live
):
    model_width = nodes.shape[1]
    node_count = nodes.shape[0]
    local_blocks = node_count // BLK
    slot_count = remote_ids.shape[1]
    row_size = lax.axis_size("row")
    col_size = lax.axis_size("col")
    my_row = lax.axis_index("row")
    my_col = lax.axis_index("col")
    self_index = my_row * col_size + my_col
    normed = normalize(nodes, ln1_gain)
    projected = jnp.dot(normed, w_qkv, preferred_element_type=jnp.float32).astype(jnp.bfloat16)
    queries = projected[:, :model_width]
    keyval = projected[:, model_width:]
    owner_dev = remote_ids // local_blocks
    local_slot = remote_ids % local_blocks
    alive_all = remote_live > 0
    same_owner = owner_dev[:, :, None] == owner_dev[:, None, :]
    slot_iota = jnp.arange(slot_count, dtype=jnp.int32)
    earlier = slot_iota[:, None] < slot_iota[None, :]
    slot_rank = jnp.sum(
        (same_owner & earlier[None] & alive_all[:, :, None]).astype(jnp.int32), axis=1
    )
    row_start = my_row * col_size
    col_pick = choose_blocks(
        lax.dynamic_slice_in_dim(owner_dev, row_start, col_size, 0),
        lax.dynamic_slice_in_dim(slot_rank, row_start, col_size, 0),
        lax.dynamic_slice_in_dim(alive_all, row_start, col_size, 0),
        lax.dynamic_slice_in_dim(local_slot, row_start, col_size, 0),
        self_index,
    )

    def column_of(table):
        return lax.dynamic_index_in_dim(
            table.reshape(row_size, col_size, slot_count), my_col, 1, keepdims=False
        )

    row_pick = choose_blocks(
        column_of(owner_dev),
        column_of(slot_rank),
        column_of(alive_all),
        column_of(local_slot),
        self_index,
    )
    source = normed.reshape(local_blocks, BLK, model_width)
    col_recv = lax.all_to_all(
        outgoing(source, col_pick, col_size), "col", split_axis=0, concat_axis=0, tiled=True
    )
    row_recv = lax.all_to_all(
        outgoing(source, row_pick, row_size), "row", split_axis=0, concat_axis=0, tiled=True
    )
    own_owner = lax.dynamic_index_in_dim(owner_dev, self_index, 0, keepdims=False)
    own_rank = jnp.minimum(
        lax.dynamic_index_in_dim(slot_rank, self_index, 0, keepdims=False), CAP - 1
    )
    own_alive = lax.dynamic_index_in_dim(remote_live, self_index, 0, keepdims=False)
    owner_row = own_owner // col_size
    owner_col = own_owner % col_size
    feature_width = col_recv.shape[3]
    from_col = jnp.take(
        col_recv.reshape(col_size * CAP, BLK, feature_width),
        owner_col * CAP + own_rank,
        axis=0,
        mode="clip",
    )
    from_row = jnp.take(
        row_recv.reshape(row_size * CAP, BLK, feature_width),
        owner_row * CAP + own_rank,
        axis=0,
        mode="clip",
    )
    gathered = jnp.where((owner_row == my_row)[:, None, None], from_col, from_row).reshape(
        slot_count * BLK, feature_width
    )
    remote_kv = jnp.dot(
        gathered, w_qkv[:, model_width:], preferred_element_type=jnp.float32
    ).astype(jnp.bfloat16)
    key_alive = jnp.repeat(own_alive, BLK)
    group_rows = 2 * BLK
    group_count = node_count // group_rows

    def one_group(pieces):
        query_part, kv_part, adj_part = pieces
        return attend(query_part, kv_part, remote_kv, adj_part, key_alive)

    mixed = lax.map(
        one_group,
        (
            queries.reshape(group_count, group_rows, model_width),
            keyval.reshape(group_count, group_rows, 2 * model_width),
            adjacency.reshape(group_count, group_rows, BLK),
        ),
    )
    mixed = mixed.reshape(node_count, model_width)
    residual = nodes.astype(jnp.float32) + jnp.dot(mixed, w_out, preferred_element_type=jnp.float32)
    normed_two = normalize(residual, ln2_gain)
    upward = jnp.dot(normed_two, w_up, preferred_element_type=jnp.float32)
    activated = jax.nn.gelu(upward, approximate=True).astype(jnp.bfloat16)
    return (residual + jnp.dot(activated, w_down, preferred_element_type=jnp.float32)).astype(
        jnp.bfloat16
    )


def solution(mesh):
    return jax.shard_map(
        shards,
        mesh=mesh,
        in_specs=(
            P(("row", "col"), None),
            P(),
            P(),
            P(),
            P(),
            P(),
            P(),
            P(("row", "col"), None),
            P(),
            P(),
        ),
        out_specs=P(("row", "col"), None),
        check_vma=False,
    )
```

profile of v0, /device:TPU:0, one launch (start us, length us, event | category | flops | bytes accessed | tf_op | source)
XLA Modules:
  0.0 227.4 jit_solution(1038354618828412443)
XLA Ops:
  0.0 1.6 copy.129
  2.2 1.3 fusion.34
  3.5 2.3 %copy.143 = bf16[1024,512]{1,0:T(8,128)(2,1)} copy(bf16[1024,512]{0,1:T(8,128)(2,1)} %fusion.34) | data formatting | bytes 2097152 | tf_op jit(solution)/shard_map/reshape | solution.py:121
  6.5 2.6 %gather_fusion.2 = bf16[4,128,512]{2,1,0:T(8,128)(2,1)} fusion(bf16[8,128,512]{2,1,0:T(8,128)(2,1)} %bitcast.131, s32[1024]{0:T(1024)S(1)} %pad_clamp_fusion.1), kind=kCustom, calls=%fused_computation.2 | custom fusion | bytes 1048592 | tf_op jit(solution)/shard_map/jit(_take)/gather | solution.py:71
  9.1 4.3 %all-to-all-start.1 = ((bf16[4,1,128,512]{3,2,1,0:T(8,128)(2,1)}), bf16[4,1,128,512]{3,2,1,0:T(8,128)(2,1)}, u32[]{:S(2)}, u32[]{:S(2)}) async-start(bf16[4,1,128,512]{3,2,1,0:T(8,128)(2,1)} %bitcast.137), calls=%async_computation.1 | async-start | bytes 1048576 | tf_op jit(solution)/shard_map/all_to_all | solution.py:125
  13.5 1.6 gather_fusion
  15.1 7.7 %all-to-all-done.1 = bf16[4,1,128,512]{3,2,1,0:T(8,128)(2,1)} async-done(((bf16[4,1,128,512]{3,2,1,0:T(8,128)(2,1)}), bf16[4,1,128,512]{3,2,1,0:T(8,128)(2,1)}, u32[]{:S(2)}, u32[]{:S(2)}) %all-to-all-start.1) | async-done | bytes 524320 | tf_op jit(solution)/shard_map/all_to_all | solution.py:125
  22.9 6.6 %all-to-all-start = ((bf16[8,1,128,512]{3,2,1,0:T(8,128)(2,1)}), bf16[8,1,128,512]{3,2,1,0:T(8,128)(2,1)S(1)}, u32[]{:S(2)}, u32[]{:S(2)}) async-start(bf16[8,1,128,512]{3,2,1,0:T(8,128)(2,1)} %bitcast.135), calls=%async_computation | async-start | bytes 2097152 | tf_op jit(solution)/shard_map/all_to_all | solution.py:122
  29.4 3.6 %convolution_convert_fusion.1 = bf16[1024,1536]{1,0:T(8,128)(2,1)S(1)} fusion(bf16[1024,512]{0,1:T(8,128)(2,1)} %fusion.34, bf16[512,1536]{1,0:T(8,128)(2,1)} %param.14), kind=kOutput, calls=%fused_computation.50 | convolution fusion | flops 1612185600 | bytes 5767168 | tf_op jit(solution)/shard_map/dot_general | solution.py:88
  33.0 1.6 slice.38
  36.1 2.8 %gather_fusion.3 = bf16[10,128,512]{2,1,0:T(8,128)(2,1)} fusion(bf16[4,128,512]{2,1,0:T(8,128)(2,1)} %bitcast.11, s32[1024]{0:T(1024)S(1)} %pad_clamp_fusion), kind=kCustom, calls=%fused_computation.3 | custom fusion | bytes 2621480 | tf_op jit(solution)/shard_map/jit(_take)/gather | solution.py:142
  39.0 16.1 %all-to-all-done = bf16[8,1,128,512]{3,2,1,0:T(8,128)(2,1)S(1)} async-done(((bf16[8,1,128,512]{3,2,1,0:T(8,128)(2,1)}), bf16[8,1,128,512]{3,2,1,0:T(8,128)(2,1)S(1)}, u32[]{:S(2)}, u32[]{:S(2)}) %all-to-all-start) | async-done | bytes 1048608 | tf_op jit(solution)/shard_map/all_to_all | solution.py:122
  55.0 1.8 gather_fusion.1
  56.8 2.1 bitcast_select_fusion
  59.0 3.0 %convolution_convert_fusion = bf16[1280,1024]{1,0:T(8,128)(2,1)} fusion(bf16[1280,512]{1,0:T(8,128)(2,1)S(1)} %bitcast_select_fusion, bf16[512,1536]{1,0:T(8,128)(2,1)S(1)} %copy-done.11), kind=kOutput, calls=%fused_computation.49 | convolution fusion | flops 1343488000 | bytes 4980736 | tf_op jit(solution)/shard_map/dot_general | solution.py:151
  62.0 4.4 %copy.136 = bf16[1280,1024]{0,1:T(8,128)(2,1)} copy(bf16[1280,1024]{1,0:T(8,128)(2,1)} %convolution_convert_fusion) | data formatting | bytes 5242880
  66.5 147.2 %while.11 = (s32[]{:T(128)}, bf16[4,256,512]{2,1,0:T(8,128)(2,1)}, bf16[4,256,1024]{2,1,0:T(8,128)(2,1)}, s32[4,256,128]{2,1,0:T(8,128)}, bf16[4,256,512]{2,1,0:...) while((s32[]{:T(128)}, bf16[4,256,512]{2,1,0:T(8,128)(2,1)}, ...), condition=%wide.region_10.11_spmd.clone, body=%wide.region_5.10_spmd.clone.sunk | while | flops 772091904 | bytes 101979416 | solution.py:162
  66.5 3.0 %fusion.88 = (bf16[1280,512]{0,1:T(8,128)(2,1)S(1)}, bf16[1280,512]{0,1:T(8,128)(2,1)}) fusion(bf16[1280,1024]{0,1:T(8,128)(2,1)} %get-tuple-element.212), kind=kLoop, calls=%fused_computation.120.clone.1 | loop fusion | bytes 5242880 | tf_op jit(solution)/shard_map/while/body/eval_jaxpr/slice | solution.py:31
  69.5 1.7 constant_dynamic-slice_fusion.4
  71.2 1.8 copy.190
  73.0 1.7 reshape.378
  74.7 6.5 %bitcast_reduce_fusion.2 = (f32[2,8,128]{2,0,1:T(2,128)S(1)}, f32[8,2,128,1280]{3,2,1,0:T(8,128)}) fusion(pred[1280]{0:T(1024)(128)(4,1)S(1)} %broadcast_bitcast_fusion.3, bf16[1280,8,64,1]{0,2,3,1:T(8,128)(2,1)S(1)} %bitcast.127, bf16[2,128,8,64]{1,0,3,2:T(2,128)(2,1)} %reshape.378), kind=kOutput, calls=%fused_computation.6.clone.1 | convolution fusion | flops 343406592 | bytes 12068096 | tf_op jit(solution)/shard_map/while/body/eval_jaxpr/bihd,jhd->bhij/dot_general | solution.py:41
  81.2 1.1 constant_dynamic-slice_fusion.5
  85.2 1.4 fusion.90
  86.8 6.4 %fusion.92 = f32[2,8,128]{2,0,1:T(2,128)S(1)} fusion(f32[8,2,128,1280]{3,2,1,0:T(8,128)} %get-tuple-element.185, f32[2,8,128]{2,0,1:T(2,128)S(1)} %copy.193, pred[1280]{0:T(1024)(128)(4,1)S(1)} %broadcast_bitcast_fusion.3), kind=kLoop, calls=%fused_computation.10.clone.1 | loop fusion | flops 10483712 | bytes 10503424 | tf_op jit(solution)/shard_map/while/body/eval_jaxpr/reduce_sum | solution.py:48
  93.8 4.2 %fusion.93 = f32[2,128,8,64]{1,3,2,0:T(8,128)} fusion(bf16[1280,8,64,1]{0,2,1,3:T(8,128)(2,1)S(1)} %bitcast.129, f32[8,2,128,1280]{3,2,1,0:T(8,128)S(1)} %copy-done.1, f32[2,8,128]{2,0,1:T(2,128)S(1)} %copy.194, f32[2,8,128]{2,0,1:T(2,128)S(1)} %copy.193, pred[1280]{0:T(1024)(128)(4,1)S(1)} %broadcast_bitcast_fusion.3), kind=kOutput, calls=%fused_computation.15.clone.1 | convolution fusion | flops 348651520 | bytes 12338432 | tf_op jit(solution)/shard_map/while/body/eval_jaxpr/bhij,jhd->bihd/dot_general | solution.py:54
  98.8 2.2 fusion.94
  100.9 1.2 copy.195
  103.3 3.0 %fusion.88 = (bf16[1280,512]{0,1:T(8,128)(2,1)S(1)}, bf16[1280,512]{0,1:T(8,128)(2,1)}) fusion(bf16[1280,1024]{0,1:T(8,128)(2,1)} %get-tuple-element.212), kind=kLoop, calls=%fused_computation.120.clone.1 | loop fusion | bytes 5242880 | tf_op jit(solution)/shard_map/while/body/eval_jaxpr/slice | solution.py:31
  106.3 1.7 constant_dynamic-slice_fusion.4
  108.0 1.8 copy.190
  109.8 1.7 reshape.378
  111.5 6.5 %bitcast_reduce_fusion.2 = (f32[2,8,128]{2,0,1:T(2,128)S(1)}, f32[8,2,128,1280]{3,2,1,0:T(8,128)}) fusion(pred[1280]{0:T(1024)(128)(4,1)S(1)} %broadcast_bitcast_fusion.3, bf16[1280,8,64,1]{0,2,3,1:T(8,128)(2,1)S(1)} %bitcast.127, bf16[2,128,8,64]{1,0,3,2:T(2,128)(2,1)} %reshape.378), kind=kOutput, calls=%fused_computation.6.clone.1 | convolution fusion | flops 343406592 | bytes 12068096 | tf_op jit(solution)/shard_map/while/body/eval_jaxpr/bihd,jhd->bhij/dot_general | solution.py:41
  118.0 1.1 constant_dynamic-slice_fusion.5
  122.0 1.4 fusion.90
  123.6 6.4 %fusion.92 = f32[2,8,128]{2,0,1:T(2,128)S(1)} fusion(f32[8,2,128,1280]{3,2,1,0:T(8,128)} %get-tuple-element.185, f32[2,8,128]{2,0,1:T(2,128)S(1)} %copy.193, pred[1280]{0:T(1024)(128)(4,1)S(1)} %broadcast_bitcast_fusion.3), kind=kLoop, calls=%fused_computation.10.clone.1 | loop fusion | flops 10483712 | bytes 10503424 | tf_op jit(solution)/shard_map/while/body/eval_jaxpr/reduce_sum | solution.py:48
  130.6 4.2 %fusion.93 = f32[2,128,8,64]{1,3,2,0:T(8,128)} fusion(bf16[1280,8,64,1]{0,2,1,3:T(8,128)(2,1)S(1)} %bitcast.129, f32[8,2,128,1280]{3,2,1,0:T(8,128)S(1)} %copy-done.1, f32[2,8,128]{2,0,1:T(2,128)S(1)} %copy.194, f32[2,8,128]{2,0,1:T(2,128)S(1)} %copy.193, pred[1280]{0:T(1024)(128)(4,1)S(1)} %broadcast_bitcast_fusion.3), kind=kOutput, calls=%fused_computation.15.clone.1 | convolution fusion | flops 348651520 | bytes 12338432 | tf_op jit(solution)/shard_map/while/body/eval_jaxpr/bhij,jhd->bihd/dot_general | solution.py:54
  135.6 2.2 fusion.94
  137.7 1.2 copy.195
  140.0 3.0 %fusion.88 = (bf16[1280,512]{0,1:T(8,128)(2,1)S(1)}, bf16[1280,512]{0,1:T(8,128)(2,1)}) fusion(bf16[1280,1024]{0,1:T(8,128)(2,1)} %get-tuple-element.212), kind=kLoop, calls=%fused_computation.120.clone.1 | loop fusion | bytes 5242880 | tf_op jit(solution)/shard_map/while/body/eval_jaxpr/slice | solution.py:31
  143.1 1.7 constant_dynamic-slice_fusion.4
  144.8 1.8 copy.190
  146.5 1.7 reshape.378
  148.3 6.5 %bitcast_reduce_fusion.2 = (f32[2,8,128]{2,0,1:T(2,128)S(1)}, f32[8,2,128,1280]{3,2,1,0:T(8,128)}) fusion(pred[1280]{0:T(1024)(128)(4,1)S(1)} %broadcast_bitcast_fusion.3, bf16[1280,8,64,1]{0,2,3,1:T(8,128)(2,1)S(1)} %bitcast.127, bf16[2,128,8,64]{1,0,3,2:T(2,128)(2,1)} %reshape.378), kind=kOutput, calls=%fused_computation.6.clone.1 | convolution fusion | flops 343406592 | bytes 12068096 | tf_op jit(solution)/shard_map/while/body/eval_jaxpr/bihd,jhd->bhij/dot_general | solution.py:41
  154.8 1.1 constant_dynamic-slice_fusion.5
  158.8 1.4 fusion.90
  160.4 6.4 %fusion.92 = f32[2,8,128]{2,0,1:T(2,128)S(1)} fusion(f32[8,2,128,1280]{3,2,1,0:T(8,128)} %get-tuple-element.185, f32[2,8,128]{2,0,1:T(2,128)S(1)} %copy.193, pred[1280]{0:T(1024)(128)(4,1)S(1)} %broadcast_bitcast_fusion.3), kind=kLoop, calls=%fused_computation.10.clone.1 | loop fusion | flops 10483712 | bytes 10503424 | tf_op jit(solution)/shard_map/while/body/eval_jaxpr/reduce_sum | solution.py:48
  167.4 4.2 %fusion.93 = f32[2,128,8,64]{1,3,2,0:T(8,128)} fusion(bf16[1280,8,64,1]{0,2,1,3:T(8,128)(2,1)S(1)} %bitcast.129, f32[8,2,128,1280]{3,2,1,0:T(8,128)S(1)} %copy-done.1, f32[2,8,128]{2,0,1:T(2,128)S(1)} %copy.194, f32[2,8,128]{2,0,1:T(2,128)S(1)} %copy.193, pred[1280]{0:T(1024)(128)(4,1)S(1)} %broadcast_bitcast_fusion.3), kind=kOutput, calls=%fused_computation.15.clone.1 | convolution fusion | flops 348651520 | bytes 12338432 | tf_op jit(solution)/shard_map/while/body/eval_jaxpr/bhij,jhd->bihd/dot_general | solution.py:54
  172.4 2.2 fusion.94
  174.5 1.2 copy.195
  176.8 3.0 %fusion.88 = (bf16[1280,512]{0,1:T(8,128)(2,1)S(1)}, bf16[1280,512]{0,1:T(8,128)(2,1)}) fusion(bf16[1280,1024]{0,1:T(8,128)(2,1)} %get-tuple-element.212), kind=kLoop, calls=%fused_computation.120.clone.1 | loop fusion | bytes 5242880 | tf_op jit(solution)/shard_map/while/body/eval_jaxpr/slice | solution.py:31
  179.9 1.7 constant_dynamic-slice_fusion.4
  181.5 1.8 copy.190
  183.3 1.7 reshape.378
  185.1 6.5 %bitcast_reduce_fusion.2 = (f32[2,8,128]{2,0,1:T(2,128)S(1)}, f32[8,2,128,1280]{3,2,1,0:T(8,128)}) fusion(pred[1280]{0:T(1024)(128)(4,1)S(1)} %broadcast_bitcast_fusion.3, bf16[1280,8,64,1]{0,2,3,1:T(8,128)(2,1)S(1)} %bitcast.127, bf16[2,128,8,64]{1,0,3,2:T(2,128)(2,1)} %reshape.378), kind=kOutput, calls=%fused_computation.6.clone.1 | convolution fusion | flops 343406592 | bytes 12068096 | tf_op jit(solution)/shard_map/while/body/eval_jaxpr/bihd,jhd->bhij/dot_general | solution.py:41
  195.6 1.4 fusion.90
  197.2 6.4 %fusion.92 = f32[2,8,128]{2,0,1:T(2,128)S(1)} fusion(f32[8,2,128,1280]{3,2,1,0:T(8,128)} %get-tuple-element.185, f32[2,8,128]{2,0,1:T(2,128)S(1)} %copy.193, pred[1280]{0:T(1024)(128)(4,1)S(1)} %broadcast_bitcast_fusion.3), kind=kLoop, calls=%fused_computation.10.clone.1 | loop fusion | flops 10483712 | bytes 10503424 | tf_op jit(solution)/shard_map/while/body/eval_jaxpr/reduce_sum | solution.py:48
  204.2 4.2 %fusion.93 = f32[2,128,8,64]{1,3,2,0:T(8,128)} fusion(bf16[1280,8,64,1]{0,2,1,3:T(8,128)(2,1)S(1)} %bitcast.129, f32[8,2,128,1280]{3,2,1,0:T(8,128)S(1)} %copy-done.1, f32[2,8,128]{2,0,1:T(2,128)S(1)} %copy.194, f32[2,8,128]{2,0,1:T(2,128)S(1)} %copy.193, pred[1280]{0:T(1024)(128)(4,1)S(1)} %broadcast_bitcast_fusion.3), kind=kOutput, calls=%fused_computation.15.clone.1 | convolution fusion | flops 348651520 | bytes 12338432 | tf_op jit(solution)/shard_map/while/body/eval_jaxpr/bhij,jhd->bihd/dot_general | solution.py:54
  209.2 2.2 fusion.94
  211.3 1.2 copy.195
  213.6 2.5 %fusion.63 = (f32[1024]{0:T(1024)S(1)}, f32[1024,512]{0,1:T(8,128)S(1)}) fusion(bf16[1024,512]{1,0:T(8,128)(2,1)} %bitcast.138, bf16[512,512]{1,0:T(8,128)(2,1)} %param.15, bf16[1024,512]{0,1:T(8,128)(2,1)} %copy-done.4), kind=kOutput, calls=%fused_computation.123 | convolution fusion | flops 538442752 | bytes 4722688 | tf_op jit(solution)/shard_map/dot_general | solution.py:171
  216.1 1.3 copy-done.6
  217.8 8.3 %add_convert_fusion = bf16[1024,512]{0,1:T(8,128)(2,1)S(1)} fusion(f32[1024,512]{0,1:T(8,128)} %copy-done.6, bf16[2048,512]{1,0:T(8,128)(2,1)S(1)} %copy-done, bf16[512,2048]{1,0:T(8,128)(2,1)} %param.17, f32[512]{0:T(512)S(1)} %copy-done.12, f32[1024]{0:T(1024)S(1)} %add_rsqrt_fusion, f32[1024]{0:T(1024)S(1)} %broadcast_multiply_fusion), kind=kOutput, calls=%fused_computation.59 | convolution fusion | flops 4316987392 | bytes 7350272 | tf_op jit(solution)/shard_map/dot_general | solution.py:175
  226.0 1.3 copy.139
  (146 shorter events, 26.1 us)
Async XLA Ops:
  0.0 217.8 %copy-start = (bf16[2048,512]{1,0:T(8,128)(2,1)S(1)}, bf16[2048,512]{1,0:T(8,128)(2,1)}, u32[]{:S(2)}) copy-start(bf16[2048,512]{1,0:T(8,128)(2,1)} %param.18) | copy-start | bytes 6291460
  0.0 2.2 copy-start.10
  1.7 1.9 copy-start.4
  2.2 3.6 %copy-start.9 = (s32[32,10]{0,1:T(8,128)S(1)}, s32[32,10]{0,1:T(8,128)}, u32[]{:S(2)}) copy-start(s32[32,10]{0,1:T(8,128)} %param.20) | copy-start | bytes 3844
  2.2 3.8 %copy-start.8 = (s32[32,10]{0,1:T(8,128)S(1)}, s32[32,10]{0,1:T(8,128)}, u32[]{:S(2)}) copy-start(s32[32,10]{0,1:T(8,128)} %param.21) | copy-start | bytes 3844
  5.8 7.7 %copy-start.7 = (bf16[1024,512]{1,0:T(8,128)(2,1)S(1)}, bf16[1024,512]{1,0:T(8,128)(2,1)}, u32[]{:S(2)}) copy-start(bf16[1024,512]{1,0:T(8,128)(2,1)} %copy.143) | copy-start | bytes 3145732
  9.1 13.7 %all-to-all-start.1 = ((bf16[4,1,128,512]{3,2,1,0:T(8,128)(2,1)}), bf16[4,1,128,512]{3,2,1,0:T(8,128)(2,1)}, u32[]{:S(2)}, u32[]{:S(2)}) async-start(bf16[4,1,128,512]{3,2,1,0:T(8,128)(2,1)} %bitcast.137), calls=%async_computation.1 | async-start | bytes 1048576 | tf_op jit(solution)/shard_map/all_to_all | solution.py:125
  22.9 32.2 %all-to-all-start = ((bf16[8,1,128,512]{3,2,1,0:T(8,128)(2,1)}), bf16[8,1,128,512]{3,2,1,0:T(8,128)(2,1)S(1)}, u32[]{:S(2)}, u32[]{:S(2)}) async-start(bf16[8,1,128,512]{3,2,1,0:T(8,128)(2,1)} %bitcast.135), calls=%async_computation | async-start | bytes 2097152 | tf_op jit(solution)/shard_map/all_to_all | solution.py:122
  56.8 2.2 copy-start.11
  81.2 4.0 %copy-start.2 = (bf16[2,128,8,64]{1,0,3,2:T(2,128)(2,1)S(1)}, bf16[2,128,8,64]{1,0,3,2:T(2,128)(2,1)}, u32[]{:S(2)}) copy-start(bf16[2,128,8,64]{1,0,3,2:T(2,128)(2,1)} %reshape.378) | copy-start | bytes 786436 | tf_op jit(solution)/shard_map/while
  85.2 8.0 %copy-start.3 = (bf16[1280,512]{0,1:T(8,128)(2,1)S(1)}, bf16[1280,512]{0,1:T(8,128)(2,1)}, u32[]{:S(2)}) copy-start(bf16[1280,512]{0,1:T(8,128)(2,1)} %get-tuple-element.183) | copy-start | bytes 3932164 | tf_op jit(solution)/shard_map/while
  86.8 7.0 %copy-start.1 = (f32[8,2,128,1280]{3,2,1,0:T(8,128)S(1)}, f32[8,2,128,1280]{3,2,1,0:T(8,128)}, u32[]{:S(2)}) copy-start(f32[8,2,128,1280]{3,2,1,0:T(8,128)} %get-tuple-element.185) | copy-start | bytes 31457284 | tf_op jit(solution)/shard_map/while
  93.8 4.2 %copy-start.5 = (bf16[256,512]{0,1:T(8,128)(2,1)S(1)}, bf16[256,512]{0,1:T(8,128)(2,1)}, u32[]{:S(2)}) copy-start(bf16[256,512]{0,1:T(8,128)(2,1)} %get-tuple-element.190) | copy-start | bytes 786436 | tf_op jit(solution)/shard_map/while
  118.0 4.0 %copy-start.2 = (bf16[2,128,8,64]{1,0,3,2:T(2,128)(2,1)S(1)}, bf16[2,128,8,64]{1,0,3,2:T(2,128)(2,1)}, u32[]{:S(2)}) copy-start(bf16[2,128,8,64]{1,0,3,2:T(2,128)(2,1)} %reshape.378) | copy-start | bytes 786436 | tf_op jit(solution)/shard_map/while
  122.0 8.1 %copy-start.3 = (bf16[1280,512]{0,1:T(8,128)(2,1)S(1)}, bf16[1280,512]{0,1:T(8,128)(2,1)}, u32[]{:S(2)}) copy-start(bf16[1280,512]{0,1:T(8,128)(2,1)} %get-tuple-element.183) | copy-start | bytes 3932164 | tf_op jit(solution)/shard_map/while
  123.6 7.0 %copy-start.1 = (f32[8,2,128,1280]{3,2,1,0:T(8,128)S(1)}, f32[8,2,128,1280]{3,2,1,0:T(8,128)}, u32[]{:S(2)}) copy-start(f32[8,2,128,1280]{3,2,1,0:T(8,128)} %get-tuple-element.185) | copy-start | bytes 31457284 | tf_op jit(solution)/shard_map/while
  130.6 4.2 %copy-start.5 = (bf16[256,512]{0,1:T(8,128)(2,1)S(1)}, bf16[256,512]{0,1:T(8,128)(2,1)}, u32[]{:S(2)}) copy-start(bf16[256,512]{0,1:T(8,128)(2,1)} %get-tuple-element.190) | copy-start | bytes 786436 | tf_op jit(solution)/shard_map/while
  154.8 4.0 %copy-start.2 = (bf16[2,128,8,64]{1,0,3,2:T(2,128)(2,1)S(1)}, bf16[2,128,8,64]{1,0,3,2:T(2,128)(2,1)}, u32[]{:S(2)}) copy-start(bf16[2,128,8,64]{1,0,3,2:T(2,128)(2,1)} %reshape.378) | copy-start | bytes 786436 | tf_op jit(solution)/shard_map/while
  158.8 8.1 %copy-start.3 = (bf16[1280,512]{0,1:T(8,128)(2,1)S(1)}, bf16[1280,512]{0,1:T(8,128)(2,1)}, u32[]{:S(2)}) copy-start(bf16[1280,512]{0,1:T(8,128)(2,1)} %get-tuple-element.183) | copy-start | bytes 3932164 | tf_op jit(solution)/shard_map/while
  160.4 7.0 %copy-start.1 = (f32[8,2,128,1280]{3,2,1,0:T(8,128)S(1)}, f32[8,2,128,1280]{3,2,1,0:T(8,128)}, u32[]{:S(2)}) copy-start(f32[8,2,128,1280]{3,2,1,0:T(8,128)} %get-tuple-element.185) | copy-start | bytes 31457284 | tf_op jit(solution)/shard_map/while
  167.4 4.2 %copy-start.5 = (bf16[256,512]{0,1:T(8,128)(2,1)S(1)}, bf16[256,512]{0,1:T(8,128)(2,1)}, u32[]{:S(2)}) copy-start(bf16[256,512]{0,1:T(8,128)(2,1)} %get-tuple-element.190) | copy-start | bytes 786436 | tf_op jit(solution)/shard_map/while
  191.6 4.0 %copy-start.2 = (bf16[2,128,8,64]{1,0,3,2:T(2,128)(2,1)S(1)}, bf16[2,128,8,64]{1,0,3,2:T(2,128)(2,1)}, u32[]{:S(2)}) copy-start(bf16[2,128,8,64]{1,0,3,2:T(2,128)(2,1)} %reshape.378) | copy-start | bytes 786436 | tf_op jit(solution)/shard_map/while
  195.6 8.1 %copy-start.3 = (bf16[1280,512]{0,1:T(8,128)(2,1)S(1)}, bf16[1280,512]{0,1:T(8,128)(2,1)}, u32[]{:S(2)}) copy-start(bf16[1280,512]{0,1:T(8,128)(2,1)} %get-tuple-element.183) | copy-start | bytes 3932164 | tf_op jit(solution)/shard_map/while
  197.2 7.0 %copy-start.1 = (f32[8,2,128,1280]{3,2,1,0:T(8,128)S(1)}, f32[8,2,128,1280]{3,2,1,0:T(8,128)}, u32[]{:S(2)}) copy-start(f32[8,2,128,1280]{3,2,1,0:T(8,128)} %get-tuple-element.185) | copy-start | bytes 31457284 | tf_op jit(solution)/shard_map/while
  204.2 4.2 %copy-start.5 = (bf16[256,512]{0,1:T(8,128)(2,1)S(1)}, bf16[256,512]{0,1:T(8,128)(2,1)}, u32[]{:S(2)}) copy-start(bf16[256,512]{0,1:T(8,128)(2,1)} %get-tuple-element.190) | copy-start | bytes 786436 | tf_op jit(solution)/shard_map/while
  216.1 1.4 copy-start.6
  216.1 1.7 copy-start.12
where the time goes:
time: 229 us; the launch traced here: 227 us
  local copies, waits for them, and re-layouts  82.4 us (36%)
  matrix products  74.7 us (33%)
  other arithmetic  35 us (15%)
  waiting for transfers between devices  23.8 us (10%)
  starting transfers between devices  10.8 us (5%)
    dot_general x4, matrix products, attend(): jnp.einsum('bihd,jhd->bhij', query_h, remote_keys, preferred_element_type...  26.2 us
    reduce_sum x8, other arithmetic, attend(): row_total = jnp.sum(local_exp, axis=-1) + jnp.sum(remote_exp, axis=-1)  26.2 us
    dynamic_slice x16, local copies, waits for them, and re-layouts, shards(): lax.map(one_group, (queries.reshape(group_count, group_rows, model_width)...  19.1 us
    dot_general x4, matrix products, attend(): jnp.einsum('bhij,jhd->bihd', remote_probs, remote_vals, preferred_element...  16.9 us
    all_to_all x1, waiting for transfers between devices, shards(): lax.all_to_all(outgoing(source, col_pick, col_size), 'col', split_axis=0,...  16.1 us
    slice x4, local copies, waits for them, and re-layouts, attend(): remote_keys = remote_kv[:, :model_width].reshape(-1, HEADS, head_dim)  11.9 us
    dynamic_update_slice x12, local copies, waits for them, and re-layouts, shards(): lax.map(one_group, (queries.reshape(group_count, group_rows, model_width)...  9.18 us
    dot_general x4, matrix products, attend(): jnp.einsum('bhij,bjhd->bihd', local_probs, local_vals, preferred_element_...  8.63 us
  transfers between devices with their start and end apart: 2, of which 2 were waited for; matrix products, arithmetic and copies ran while one was open for 5% of the time, Pallas kernels for 0%

commit v1 on v0

--- a/solution.py
+++ b/solution.py
@@ -9,6 +9,29 @@
 CAP = 1
 EPS = 1e-05
 NEG_FILL = -1e30
+
+
+def cut_along(shard, dim, size):
+    dims = shard.shape
+    blocks = shard.reshape(*dims[:dim], size, dims[dim] // size, *dims[dim + 1 :])
+    return jnp.moveaxis(blocks, dim, 0)
+
+
+def joined_along(pieces, dim):
+    pieces = jnp.moveaxis(pieces, 0, dim)
+    dims = pieces.shape
+    return pieces.reshape(*dims[:dim], dims[dim] * dims[dim + 1], *dims[dim + 2 :])
+
+
+def swapped_with_each(x, axis, split_dim, concat_dim):
+    size, position = (lax.axis_size(axis), lax.axis_index(axis))
+    pieces = cut_along(x, split_dim, size)
+    outs = [pieces[position]]
+    for step in range(1, size):
+        sent = pieces[position ^ step]
+        outs.append(lax.ppermute(sent, axis, [(i, i ^ step) for i in range(size)]))
+    pieces = jnp.stack(outs)[position ^ jnp.arange(size)]
+    return joined_along(pieces, concat_dim)
 
 
 def normalize(values, gain):
@@ -122,9 +145,7 @@
     col_recv = lax.all_to_all(
         outgoing(source, col_pick, col_size), "col", split_axis=0, concat_axis=0, tiled=True
     )
-    row_recv = lax.all_to_all(
-        outgoing(source, row_pick, row_size), "row", split_axis=0, concat_axis=0, tiled=True
-    )
+    row_recv = swapped_with_each(outgoing(source, row_pick, row_size), "row", 0, 0)
     own_owner = lax.dynamic_index_in_dim(owner_dev, self_index, 0, keepdims=False)
     own_rank = jnp.minimum(
         lax.dynamic_index_in_dim(slot_rank, self_index, 0, keepdims=False), CAP - 1

time: 229 us -> 217 us (0.948)
  waiting for transfers between devices: 23.8 us -> 7.29 us
  local copies, waits for them, and re-layouts: 82.4 us -> 87 us
    all_to_all x1, waiting for transfers between devices: 16.1 us -> 7.28 us  [shards(): lax.all_to_all(outgoing(source, col_pick, col_size), 'col', split_axis=0,...]
    all_to_all x1 -> x0, waiting for transfers between devices: 7.71 us -> none  [shards(): lax.all_to_all(outgoing(source, row_pick, row_size), 'row', split_axis=0,...]
    all_to_all x1 -> x0, starting transfers between devices: 4.27 us -> none  [shards(): lax.all_to_all(outgoing(source, row_pick, row_size), 'row', split_axis=0,...]
    unnamed x20 -> x22, local copies, waits for them, and re-layouts: 7.54 us -> 7.48 us
  transfers between devices with their start and end apart: 2 -> 4, of which waited for: 2 -> 1; matrix products, arithmetic and copies ran while one was open for 5% -> 8% of each run, Pallas kernels for 0% -> 0%
where the time goes in v1:
time: 217 us; the launch traced here: 215 us
  local copies, waits for them, and re-layouts  87 us (40%)
  matrix products  76.3 us (35%)
  other arithmetic  34.7 us (16%)
  starting transfers between devices  9.21 us (4%)
  waiting for transfers between devices  7.29 us (3%)
    dot_general x4, matrix products, attend(): jnp.einsum('bihd,jhd->bhij', query_h, remote_keys, preferred_element_type...  26.2 us
    reduce_sum x8, other arithmetic, attend(): row_total = jnp.sum(local_exp, axis=-1) + jnp.sum(remote_exp, axis=-1)  26.2 us
    dynamic_slice x16, local copies, waits for them, and re-layouts, shards(): lax.map(one_group, (queries.reshape(group_count, group_rows, model_width)...  19.1 us
    dot_general x4, matrix products, attend(): jnp.einsum('bhij,jhd->bihd', remote_probs, remote_vals, preferred_element...  16.9 us
    slice x4, local copies, waits for them, and re-layouts, attend(): remote_keys = remote_kv[:, :model_width].reshape(-1, HEADS, head_dim)  11.9 us
    dynamic_update_slice x12, local copies, waits for them, and re-layouts, shards(): lax.map(one_group, (queries.reshape(group_count, group_rows, model_width)...  9.18 us
    dot_general x4, matrix products, attend(): jnp.einsum('bhij,bjhd->bihd', local_probs, local_vals, preferred_element_...  8.63 us
    dot_general x1, matrix products, shards(): jnp.dot(activated, w_down, preferred_element_type=jnp.float32)  8.26 us
  transfers between devices with their start and end apart: 4, of which 1 were waited for; matrix products, arithmetic and copies ran while one was open for 8% of the time, Pallas kernels for 0%

profile of v1, /device:TPU:0, one launch (start us, length us, event | category | flops | bytes accessed | tf_op | source)
XLA Modules:
  0.0 215.3 jit_solution(11031788997186374682)
XLA Ops:
  0.0 1.6 copy.127
  2.2 1.3 fusion.34
  3.5 2.3 %copy.140 = bf16[1024,512]{1,0:T(8,128)(2,1)} copy(bf16[1024,512]{0,1:T(8,128)(2,1)} %fusion.34) | data formatting | bytes 2097152 | tf_op jit(solution)/shard_map/reshape | solution.py:144
  6.1 2.9 %gather_fusion = bf16[8,128,512]{2,1,0:T(8,128)(2,1)} fusion(bf16[8,128,512]{2,1,0:T(8,128)(2,1)} %bitcast.142, s32[1024]{0:T(1024)S(1)} %pad_clamp_fusion.4), kind=kCustom, calls=%fused_computation | custom fusion | bytes 2097184 | tf_op jit(solution)/shard_map/jit(_take)/gather | solution.py:94
  9.0 7.3 %all-to-all-start = ((bf16[8,1,128,512]{3,2,1,0:T(8,128)(2,1)}), bf16[8,1,128,512]{3,2,1,0:T(8,128)(2,1)}, u32[]{:S(2)}, u32[]{:S(2)}) async-start(bf16[8,1,128,512]{3,2,1,0:T(8,128)(2,1)} %bitcast.145), calls=%async_computation | async-start | bytes 2097152 | tf_op jit(solution)/shard_map/all_to_all | solution.py:145
  16.9 1.4 gather_fusion.2
  18.2 1.1 dynamic-slice_bitcast_fusion.3
  21.6 5.2 %convolution_convert_fusion.1 = bf16[1024,1536]{1,0:T(8,128)(2,1)} fusion(bf16[1024,512]{0,1:T(8,128)(2,1)} %fusion.34, bf16[512,1536]{1,0:T(8,128)(2,1)} %param.14), kind=kOutput, calls=%fused_computation.51 | convolution fusion | flops 1612185600 | bytes 5767168 | tf_op jit(solution)/shard_map/dot_general | solution.py:111
  26.8 3.1 %slice.40 = bf16[1024,1024]{1,0:T(8,128)(2,1)} slice(bf16[1024,1536]{1,0:T(8,128)(2,1)} %convolution_convert_fusion.1), slice={[0:1024], [512:1536]} | slice | bytes 4194304 | tf_op jit(solution)/shard_map/slice | solution.py:113
  29.9 2.3 %slice.41 = bf16[1024,512]{1,0:T(8,128)(2,1)} slice(bf16[1024,1536]{1,0:T(8,128)(2,1)} %convolution_convert_fusion.1), slice={[0:1024], [0:512]} | slice | bytes 2097152 | tf_op jit(solution)/shard_map/slice | solution.py:112
  33.1 1.8 gather_fusion.4
  34.9 7.3 %all-to-all-done = bf16[8,1,128,512]{3,2,1,0:T(8,128)(2,1)} async-done(((bf16[8,1,128,512]{3,2,1,0:T(8,128)(2,1)}), bf16[8,1,128,512]{3,2,1,0:T(8,128)(2,1)}, u32[]{:S(2)}, u32[]{:S(2)}) %all-to-all-start) | async-done | bytes 1048608 | tf_op jit(solution)/shard_map/all_to_all | solution.py:145
  42.1 3.0 %gather_fusion.1 = bf16[10,128,512]{2,1,0:T(8,128)(2,1)} fusion(bf16[8,128,512]{2,1,0:T(8,128)(2,1)} %bitcast.6, s32[1024]{0:T(1024)S(1)} %pad_clamp_fusion.3), kind=kCustom, calls=%fused_computation.1 | custom fusion | bytes 2621480 | tf_op jit(solution)/shard_map/jit(_take)/gather | solution.py:157
  45.2 1.7 bitcast_select_fusion
  47.0 3.0 %convolution_convert_fusion = bf16[1280,1024]{1,0:T(8,128)(2,1)} fusion(bf16[1280,512]{1,0:T(8,128)(2,1)S(1)} %bitcast_select_fusion, bf16[512,1536]{1,0:T(8,128)(2,1)S(1)} %copy-done.12), kind=kOutput, calls=%fused_computation.50 | convolution fusion | flops 1343488000 | bytes 4980736 | tf_op jit(solution)/shard_map/dot_general | solution.py:172
  50.0 4.4 %copy.133 = bf16[1280,1024]{0,1:T(8,128)(2,1)} copy(bf16[1280,1024]{1,0:T(8,128)(2,1)} %convolution_convert_fusion) | data formatting | bytes 5242880
  54.4 147.2 %while.11 = (s32[]{:T(128)}, bf16[4,256,512]{2,1,0:T(8,128)(2,1)}, bf16[4,256,1024]{2,1,0:T(8,128)(2,1)}, s32[4,256,128]{2,1,0:T(8,128)}, bf16[4,256,512]{2,1,0:...) while((s32[]{:T(128)}, bf16[4,256,512]{2,1,0:T(8,128)(2,1)}, ...), condition=%wide.region_10.11_spmd.clone, body=%wide.region_5.10_spmd.clone.sunk | while | flops 772091904 | bytes 101979416 | solution.py:183
  54.4 3.0 %fusion.89 = (bf16[1280,512]{0,1:T(8,128)(2,1)S(1)}, bf16[1280,512]{0,1:T(8,128)(2,1)}) fusion(bf16[1280,1024]{0,1:T(8,128)(2,1)} %get-tuple-element.216), kind=kLoop, calls=%fused_computation.129.clone.1 | loop fusion | bytes 5242880 | tf_op jit(solution)/shard_map/while/body/eval_jaxpr/slice | solution.py:54
  57.5 1.7 constant_dynamic-slice_fusion.4
  59.1 1.8 copy.187
  60.9 1.7 reshape.408
  62.6 6.5 %bitcast_reduce_fusion.2 = (f32[2,8,128]{2,0,1:T(2,128)S(1)}, f32[8,2,128,1280]{3,2,1,0:T(8,128)}) fusion(pred[1280]{0:T(1024)(128)(4,1)S(1)} %broadcast_bitcast_fusion.3, bf16[1280,8,64,1]{0,2,3,1:T(8,128)(2,1)S(1)} %bitcast.138, bf16[2,128,8,64]{1,0,3,2:T(2,128)(2,1)} %reshape.408), kind=kOutput, calls=%fused_computation.7.clone.1 | convolution fusion | flops 343406592 | bytes 12068096 | tf_op jit(solution)/shard_map/while/body/eval_jaxpr/bihd,jhd->bhij/dot_general | solution.py:64
  69.2 1.1 constant_dynamic-slice_fusion.5
  73.2 1.4 fusion.91
  74.8 6.4 %fusion.93 = f32[2,8,128]{2,0,1:T(2,128)S(1)} fusion(f32[8,2,128,1280]{3,2,1,0:T(8,128)} %get-tuple-element.189, f32[2,8,128]{2,0,1:T(2,128)S(1)} %copy.190, pred[1280]{0:T(1024)(128)(4,1)S(1)} %broadcast_bitcast_fusion.3), kind=kLoop, calls=%fused_computation.11.clone.1 | loop fusion | flops 10483712 | bytes 10503424 | tf_op jit(solution)/shard_map/while/body/eval_jaxpr/reduce_sum | solution.py:71
  81.7 4.2 %fusion.94 = f32[2,128,8,64]{1,3,2,0:T(8,128)} fusion(bf16[1280,8,64,1]{0,2,1,3:T(8,128)(2,1)S(1)} %bitcast.140, f32[8,2,128,1280]{3,2,1,0:T(8,128)S(1)} %copy-done.1, f32[2,8,128]{2,0,1:T(2,128)S(1)} %copy.191, f32[2,8,128]{2,0,1:T(2,128)S(1)} %copy.190, pred[1280]{0:T(1024)(128)(4,1)S(1)} %broadcast_bitcast_fusion.3), kind=kOutput, calls=%fused_computation.16.clone.1 | convolution fusion | flops 348651520 | bytes 12338432 | tf_op jit(solution)/shard_map/while/body/eval_jaxpr/bhij,jhd->bihd/dot_general | solution.py:77
  86.7 2.2 %fusion.95 = bf16[2,128,8,64]{1,3,2,0:T(8,128)(2,1)} fusion(f32[2,128,8,64]{1,3,2,0:T(8,128)} %fusion.94, f32[2,8,128,128]{2,3,1,0:T(8,128)S(1)} %get-tuple-element.191, f32[2,8,128]{2,1,0:T(8,128)S(1)} %copy_add_fusion.2, f32[2,8,128]{2,1,0:T(8,128)S(1)} %copy_maximum_fusion.2, bf16[2,128,8,64]{1,0,3,2:T(2,128)(2,1)} %reshape.410), kind=kOutput, calls=%fused_computation.19.clone.1 | convolution fusion | flops 34603008 | bytes 2113536 | tf_op jit(solution)/shard_map/while/body/eval_jaxpr/bhij,bjhd->bihd/dot_general | solution.py:74
  88.9 1.2 copy.192
  91.2 3.0 %fusion.89 = (bf16[1280,512]{0,1:T(8,128)(2,1)S(1)}, bf16[1280,512]{0,1:T(8,128)(2,1)}) fusion(bf16[1280,1024]{0,1:T(8,128)(2,1)} %get-tuple-element.216), kind=kLoop, calls=%fused_computation.129.clone.1 | loop fusion | bytes 5242880 | tf_op jit(solution)/shard_map/while/body/eval_jaxpr/slice | solution.py:54
  94.3 1.7 constant_dynamic-slice_fusion.4
  95.9 1.8 copy.187
  97.7 1.7 reshape.408
  99.4 6.5 %bitcast_reduce_fusion.2 = (f32[2,8,128]{2,0,1:T(2,128)S(1)}, f32[8,2,128,1280]{3,2,1,0:T(8,128)}) fusion(pred[1280]{0:T(1024)(128)(4,1)S(1)} %broadcast_bitcast_fusion.3, bf16[1280,8,64,1]{0,2,3,1:T(8,128)(2,1)S(1)} %bitcast.138, bf16[2,128,8,64]{1,0,3,2:T(2,128)(2,1)} %reshape.408), kind=kOutput, calls=%fused_computation.7.clone.1 | convolution fusion | flops 343406592 | bytes 12068096 | tf_op jit(solution)/shard_map/while/body/eval_jaxpr/bihd,jhd->bhij/dot_general | solution.py:64
  106.0 1.1 constant_dynamic-slice_fusion.5
  110.0 1.4 fusion.91
  111.6 6.4 %fusion.93 = f32[2,8,128]{2,0,1:T(2,128)S(1)} fusion(f32[8,2,128,1280]{3,2,1,0:T(8,128)} %get-tuple-element.189, f32[2,8,128]{2,0,1:T(2,128)S(1)} %copy.190, pred[1280]{0:T(1024)(128)(4,1)S(1)} %broadcast_bitcast_fusion.3), kind=kLoop, calls=%fused_computation.11.clone.1 | loop fusion | flops 10483712 | bytes 10503424 | tf_op jit(solution)/shard_map/while/body/eval_jaxpr/reduce_sum | solution.py:71
  118.5 4.2 %fusion.94 = f32[2,128,8,64]{1,3,2,0:T(8,128)} fusion(bf16[1280,8,64,1]{0,2,1,3:T(8,128)(2,1)S(1)} %bitcast.140, f32[8,2,128,1280]{3,2,1,0:T(8,128)S(1)} %copy-done.1, f32[2,8,128]{2,0,1:T(2,128)S(1)} %copy.191, f32[2,8,128]{2,0,1:T(2,128)S(1)} %copy.190, pred[1280]{0:T(1024)(128)(4,1)S(1)} %broadcast_bitcast_fusion.3), kind=kOutput, calls=%fused_computation.16.clone.1 | convolution fusion | flops 348651520 | bytes 12338432 | tf_op jit(solution)/shard_map/while/body/eval_jaxpr/bhij,jhd->bihd/dot_general | solution.py:77
  123.5 2.2 %fusion.95 = bf16[2,128,8,64]{1,3,2,0:T(8,128)(2,1)} fusion(f32[2,128,8,64]{1,3,2,0:T(8,128)} %fusion.94, f32[2,8,128,128]{2,3,1,0:T(8,128)S(1)} %get-tuple-element.191, f32[2,8,128]{2,1,0:T(8,128)S(1)} %copy_add_fusion.2, f32[2,8,128]{2,1,0:T(8,128)S(1)} %copy_maximum_fusion.2, bf16[2,128,8,64]{1,0,3,2:T(2,128)(2,1)} %reshape.410), kind=kOutput, calls=%fused_computation.19.clone.1 | convolution fusion | flops 34603008 | bytes 2113536 | tf_op jit(solution)/shard_map/while/body/eval_jaxpr/bhij,bjhd->bihd/dot_general | solution.py:74
  125.7 1.2 copy.192
  128.0 3.0 %fusion.89 = (bf16[1280,512]{0,1:T(8,128)(2,1)S(1)}, bf16[1280,512]{0,1:T(8,128)(2,1)}) fusion(bf16[1280,1024]{0,1:T(8,128)(2,1)} %get-tuple-element.216), kind=kLoop, calls=%fused_computation.129.clone.1 | loop fusion | bytes 5242880 | tf_op jit(solution)/shard_map/while/body/eval_jaxpr/slice | solution.py:54
  131.1 1.7 constant_dynamic-slice_fusion.4
  132.7 1.8 copy.187
  134.5 1.7 reshape.408
  136.2 6.5 %bitcast_reduce_fusion.2 = (f32[2,8,128]{2,0,1:T(2,128)S(1)}, f32[8,2,128,1280]{3,2,1,0:T(8,128)}) fusion(pred[1280]{0:T(1024)(128)(4,1)S(1)} %broadcast_bitcast_fusion.3, bf16[1280,8,64,1]{0,2,3,1:T(8,128)(2,1)S(1)} %bitcast.138, bf16[2,128,8,64]{1,0,3,2:T(2,128)(2,1)} %reshape.408), kind=kOutput, calls=%fused_computation.7.clone.1 | convolution fusion | flops 343406592 | bytes 12068096 | tf_op jit(solution)/shard_map/while/body/eval_jaxpr/bihd,jhd->bhij/dot_general | solution.py:64
  146.8 1.4 fusion.91
  148.4 6.4 %fusion.93 = f32[2,8,128]{2,0,1:T(2,128)S(1)} fusion(f32[8,2,128,1280]{3,2,1,0:T(8,128)} %get-tuple-element.189, f32[2,8,128]{2,0,1:T(2,128)S(1)} %copy.190, pred[1280]{0:T(1024)(128)(4,1)S(1)} %broadcast_bitcast_fusion.3), kind=kLoop, calls=%fused_computation.11.clone.1 | loop fusion | flops 10483712 | bytes 10503424 | tf_op jit(solution)/shard_map/while/body/eval_jaxpr/reduce_sum | solution.py:71
  155.3 4.2 %fusion.94 = f32[2,128,8,64]{1,3,2,0:T(8,128)} fusion(bf16[1280,8,64,1]{0,2,1,3:T(8,128)(2,1)S(1)} %bitcast.140, f32[8,2,128,1280]{3,2,1,0:T(8,128)S(1)} %copy-done.1, f32[2,8,128]{2,0,1:T(2,128)S(1)} %copy.191, f32[2,8,128]{2,0,1:T(2,128)S(1)} %copy.190, pred[1280]{0:T(1024)(128)(4,1)S(1)} %broadcast_bitcast_fusion.3), kind=kOutput, calls=%fused_computation.16.clone.1 | convolution fusion | flops 348651520 | bytes 12338432 | tf_op jit(solution)/shard_map/while/body/eval_jaxpr/bhij,jhd->bihd/dot_general | solution.py:77
  160.3 2.2 %fusion.95 = bf16[2,128,8,64]{1,3,2,0:T(8,128)(2,1)} fusion(f32[2,128,8,64]{1,3,2,0:T(8,128)} %fusion.94, f32[2,8,128,128]{2,3,1,0:T(8,128)S(1)} %get-tuple-element.191, f32[2,8,128]{2,1,0:T(8,128)S(1)} %copy_add_fusion.2, f32[2,8,128]{2,1,0:T(8,128)S(1)} %copy_maximum_fusion.2, bf16[2,128,8,64]{1,0,3,2:T(2,128)(2,1)} %reshape.410), kind=kOutput, calls=%fused_computation.19.clone.1 | convolution fusion | flops 34603008 | bytes 2113536 | tf_op jit(solution)/shard_map/while/body/eval_jaxpr/bhij,bjhd->bihd/dot_general | solution.py:74
  162.5 1.2 copy.192
  164.8 3.0 %fusion.89 = (bf16[1280,512]{0,1:T(8,128)(2,1)S(1)}, bf16[1280,512]{0,1:T(8,128)(2,1)}) fusion(bf16[1280,1024]{0,1:T(8,128)(2,1)} %get-tuple-element.216), kind=kLoop, calls=%fused_computation.129.clone.1 | loop fusion | bytes 5242880 | tf_op jit(solution)/shard_map/while/body/eval_jaxpr/slice | solution.py:54
  167.8 1.7 constant_dynamic-slice_fusion.4
  169.5 1.8 copy.187
  171.3 1.7 reshape.408
  173.0 6.5 %bitcast_reduce_fusion.2 = (f32[2,8,128]{2,0,1:T(2,128)S(1)}, f32[8,2,128,1280]{3,2,1,0:T(8,128)}) fusion(pred[1280]{0:T(1024)(128)(4,1)S(1)} %broadcast_bitcast_fusion.3, bf16[1280,8,64,1]{0,2,3,1:T(8,128)(2,1)S(1)} %bitcast.138, bf16[2,128,8,64]{1,0,3,2:T(2,128)(2,1)} %reshape.408), kind=kOutput, calls=%fused_computation.7.clone.1 | convolution fusion | flops 343406592 | bytes 12068096 | tf_op jit(solution)/shard_map/while/body/eval_jaxpr/bihd,jhd->bhij/dot_general | solution.py:64
  179.6 1.1 constant_dynamic-slice_fusion.5
  183.5 1.4 fusion.91
  185.2 6.4 %fusion.93 = f32[2,8,128]{2,0,1:T(2,128)S(1)} fusion(f32[8,2,128,1280]{3,2,1,0:T(8,128)} %get-tuple-element.189, f32[2,8,128]{2,0,1:T(2,128)S(1)} %copy.190, pred[1280]{0:T(1024)(128)(4,1)S(1)} %broadcast_bitcast_fusion.3), kind=kLoop, calls=%fused_computation.11.clone.1 | loop fusion | flops 10483712 | bytes 10503424 | tf_op jit(solution)/shard_map/while/body/eval_jaxpr/reduce_sum | solution.py:71
  192.1 4.2 %fusion.94 = f32[2,128,8,64]{1,3,2,0:T(8,128)} fusion(bf16[1280,8,64,1]{0,2,1,3:T(8,128)(2,1)S(1)} %bitcast.140, f32[8,2,128,1280]{3,2,1,0:T(8,128)S(1)} %copy-done.1, f32[2,8,128]{2,0,1:T(2,128)S(1)} %copy.191, f32[2,8,128]{2,0,1:T(2,128)S(1)} %copy.190, pred[1280]{0:T(1024)(128)(4,1)S(1)} %broadcast_bitcast_fusion.3), kind=kOutput, calls=%fused_computation.16.clone.1 | convolution fusion | flops 348651520 | bytes 12338432 | tf_op jit(solution)/shard_map/while/body/eval_jaxpr/bhij,jhd->bihd/dot_general | solution.py:77
  197.1 2.2 %fusion.95 = bf16[2,128,8,64]{1,3,2,0:T(8,128)(2,1)} fusion(f32[2,128,8,64]{1,3,2,0:T(8,128)} %fusion.94, f32[2,8,128,128]{2,3,1,0:T(8,128)S(1)} %get-tuple-element.191, f32[2,8,128]{2,1,0:T(8,128)S(1)} %copy_add_fusion.2, f32[2,8,128]{2,1,0:T(8,128)S(1)} %copy_maximum_fusion.2, bf16[2,128,8,64]{1,0,3,2:T(2,128)(2,1)} %reshape.410), kind=kOutput, calls=%fused_computation.19.clone.1 | convolution fusion | flops 34603008 | bytes 2113536 | tf_op jit(solution)/shard_map/while/body/eval_jaxpr/bhij,bjhd->bihd/dot_general | solution.py:74
  199.3 1.2 copy.192
  201.6 2.5 %fusion.64 = (f32[1024]{0:T(1024)S(1)}, f32[1024,512]{0,1:T(8,128)S(1)}) fusion(bf16[1024,512]{1,0:T(8,128)(2,1)} %bitcast.147, bf16[512,512]{1,0:T(8,128)(2,1)} %param.15, bf16[1024,512]{0,1:T(8,128)(2,1)} %copy-done.4), kind=kOutput, calls=%fused_computation.132 | convolution fusion | flops 538442752 | bytes 4722688 | tf_op jit(solution)/shard_map/dot_general | solution.py:192
  204.1 1.3 copy-done.6
  205.7 8.3 %add_convert_fusion = bf16[1024,512]{0,1:T(8,128)(2,1)S(1)} fusion(f32[1024,512]{0,1:T(8,128)} %copy-done.6, bf16[2048,512]{1,0:T(8,128)(2,1)S(1)} %copy-done, bf16[512,2048]{1,0:T(8,128)(2,1)} %param.17, f32[512]{0:T(512)S(1)} %copy-done.13, f32[1024]{0:T(1024)S(1)} %add_rsqrt_fusion, f32[1024]{0:T(1024)S(1)} %broadcast_multiply_fusion), kind=kOutput, calls=%fused_computation.60 | convolution fusion | flops 4316987392 | bytes 7350272 | tf_op jit(solution)/shard_map/dot_general | solution.py:196
  214.0 1.3 copy.136
  (157 shorter events, 27.6 us)
Async XLA Ops:
  0.0 205.7 %copy-start = (bf16[2048,512]{1,0:T(8,128)(2,1)S(1)}, bf16[2048,512]{1,0:T(8,128)(2,1)}, u32[]{:S(2)}) copy-start(bf16[2048,512]{1,0:T(8,128)(2,1)} %param.18) | copy-start | bytes 6291460
  0.0 2.2 %copy-start.11 = (f32[512]{0:T(512)S(1)}, f32[512]{0:T(512)}, u32[]{:S(2)}) copy-start(f32[512]{0:T(512)} %param.13) | copy-start | bytes 6148
  1.7 1.9 copy-start.4
  2.2 3.6 %copy-start.10 = (s32[32,10]{0,1:T(8,128)S(1)}, s32[32,10]{0,1:T(8,128)}, u32[]{:S(2)}) copy-start(s32[32,10]{0,1:T(8,128)} %param.20) | copy-start | bytes 3844
  2.2 3.6 %copy-start.9 = (s32[32,10]{0,1:T(8,128)S(1)}, s32[32,10]{0,1:T(8,128)}, u32[]{:S(2)}) copy-start(s32[32,10]{0,1:T(8,128)} %param.21) | copy-start | bytes 3844
  6.1 10.8 %copy-start.7 = (bf16[1024,512]{1,0:T(8,128)(2,1)S(1)}, bf16[1024,512]{1,0:T(8,128)(2,1)}, u32[]{:S(2)}) copy-start(bf16[1024,512]{1,0:T(8,128)(2,1)} %copy.140) | copy-start | bytes 3145732
  9.0 33.2 %all-to-all-start = ((bf16[8,1,128,512]{3,2,1,0:T(8,128)(2,1)}), bf16[8,1,128,512]{3,2,1,0:T(8,128)(2,1)}, u32[]{:S(2)}, u32[]{:S(2)}) async-start(bf16[8,1,128,512]{3,2,1,0:T(8,128)(2,1)} %bitcast.145), calls=%async_computation | async-start | bytes 2097152 | tf_op jit(solution)/shard_map/all_to_all | solution.py:145
  19.4 13.0 %collective-permute-start.2 = (bf16[1,1,128,512]{3,2,1,0:T(8,128)(2,1)S(1)}, bf16[1,1,128,512]{3,2,1,0:T(8,128)(2,1)S(1)}, u32[]{:S(2)}, u32[]{:S(2)}) collective-permute-start(bf16[1,1,128,512]{3,2,1,0:T(8,128)(2,1)S(1)} %get-tuple-element.127), channel_id=1, source_target_pairs={{0,24},{8,16},{16,8},{24,0},{1,25},{9,17},{17,9},{25,1},{2,26},{10... | collective-permute-start | bytes 393224 | tf_op jit(solution)/shard_map/ppermute | solution.py:32
  20.1 12.3 %collective-permute-start.1 = (bf16[1,1,128,512]{3,2,1,0:T(8,128)(2,1)S(1)}, bf16[1,1,128,512]{3,2,1,0:T(8,128)(2,1)S(1)}, u32[]{:S(2)}, u32[]{:S(2)}) collective-permute-start(bf16[1,1,128,512]{3,2,1,0:T(8,128)(2,1)S(1)} %get-tuple-element.125), channel_id=1, source_target_pairs={{0,16},{8,24},{16,0},{24,8},{1,17},{9,25},{17,1},{25,9},{2,18},{10... | collective-permute-start | bytes 393224 | tf_op jit(solution)/shard_map/ppermute | solution.py:32
  21.0 11.4 %collective-permute-start = (bf16[1,1,128,512]{3,2,1,0:T(8,128)(2,1)S(1)}, bf16[1,1,128,512]{3,2,1,0:T(8,128)(2,1)S(1)}, u32[]{:S(2)}, u32[]{:S(2)}) collective-permute-start(bf16[1,1,128,512]{3,2,1,0:T(8,128)(2,1)S(1)} %get-tuple-element.126), channel_id=1, source_target_pairs={{0,8},{8,0},{16,24},{24,16},{1,9},{9,1},{17,25},{25,17},{2,10},{10... | collective-permute-start | bytes 393224 | tf_op jit(solution)/shard_map/ppermute | solution.py:32
  34.9 10.3 %copy-start.8 = (bf16[10,128,512]{2,1,0:T(8,128)(2,1)S(1)}, bf16[10,128,512]{2,1,0:T(8,128)(2,1)}, u32[]{:S(2)}) copy-start(bf16[10,128,512]{2,1,0:T(8,128)(2,1)} %gather_fusion.4) | copy-start | bytes 3932164
  45.2 1.8 copy-start.12
  69.2 4.0 %copy-start.2 = (bf16[2,128,8,64]{1,0,3,2:T(2,128)(2,1)S(1)}, bf16[2,128,8,64]{1,0,3,2:T(2,128)(2,1)}, u32[]{:S(2)}) copy-start(bf16[2,128,8,64]{1,0,3,2:T(2,128)(2,1)} %reshape.408) | copy-start | bytes 786436 | tf_op jit(solution)/shard_map/while
  73.2 8.0 %copy-start.3 = (bf16[1280,512]{0,1:T(8,128)(2,1)S(1)}, bf16[1280,512]{0,1:T(8,128)(2,1)}, u32[]{:S(2)}) copy-start(bf16[1280,512]{0,1:T(8,128)(2,1)} %get-tuple-element.187) | copy-start | bytes 3932164 | tf_op jit(solution)/shard_map/while
  74.8 7.0 %copy-start.1 = (f32[8,2,128,1280]{3,2,1,0:T(8,128)S(1)}, f32[8,2,128,1280]{3,2,1,0:T(8,128)}, u32[]{:S(2)}) copy-start(f32[8,2,128,1280]{3,2,1,0:T(8,128)} %get-tuple-element.189) | copy-start | bytes 31457284 | tf_op jit(solution)/shard_map/while
  81.7 4.2 %copy-start.5 = (bf16[256,512]{0,1:T(8,128)(2,1)S(1)}, bf16[256,512]{0,1:T(8,128)(2,1)}, u32[]{:S(2)}) copy-start(bf16[256,512]{0,1:T(8,128)(2,1)} %get-tuple-element.194) | copy-start | bytes 786436 | tf_op jit(solution)/shard_map/while
  106.0 4.0 %copy-start.2 = (bf16[2,128,8,64]{1,0,3,2:T(2,128)(2,1)S(1)}, bf16[2,128,8,64]{1,0,3,2:T(2,128)(2,1)}, u32[]{:S(2)}) copy-start(bf16[2,128,8,64]{1,0,3,2:T(2,128)(2,1)} %reshape.408) | copy-start | bytes 786436 | tf_op jit(solution)/shard_map/while
  110.0 8.1 %copy-start.3 = (bf16[1280,512]{0,1:T(8,128)(2,1)S(1)}, bf16[1280,512]{0,1:T(8,128)(2,1)}, u32[]{:S(2)}) copy-start(bf16[1280,512]{0,1:T(8,128)(2,1)} %get-tuple-element.187) | copy-start | bytes 3932164 | tf_op jit(solution)/shard_map/while
  111.6 7.0 %copy-start.1 = (f32[8,2,128,1280]{3,2,1,0:T(8,128)S(1)}, f32[8,2,128,1280]{3,2,1,0:T(8,128)}, u32[]{:S(2)}) copy-start(f32[8,2,128,1280]{3,2,1,0:T(8,128)} %get-tuple-element.189) | copy-start | bytes 31457284 | tf_op jit(solution)/shard_map/while
  118.5 4.2 %copy-start.5 = (bf16[256,512]{0,1:T(8,128)(2,1)S(1)}, bf16[256,512]{0,1:T(8,128)(2,1)}, u32[]{:S(2)}) copy-start(bf16[256,512]{0,1:T(8,128)(2,1)} %get-tuple-element.194) | copy-start | bytes 786436 | tf_op jit(solution)/shard_map/while
  142.8 4.0 %copy-start.2 = (bf16[2,128,8,64]{1,0,3,2:T(2,128)(2,1)S(1)}, bf16[2,128,8,64]{1,0,3,2:T(2,128)(2,1)}, u32[]{:S(2)}) copy-start(bf16[2,128,8,64]{1,0,3,2:T(2,128)(2,1)} %reshape.408) | copy-start | bytes 786436 | tf_op jit(solution)/shard_map/while
  146.7 8.1 %copy-start.3 = (bf16[1280,512]{0,1:T(8,128)(2,1)S(1)}, bf16[1280,512]{0,1:T(8,128)(2,1)}, u32[]{:S(2)}) copy-start(bf16[1280,512]{0,1:T(8,128)(2,1)} %get-tuple-element.187) | copy-start | bytes 3932164 | tf_op jit(solution)/shard_map/while
  148.4 7.0 %copy-start.1 = (f32[8,2,128,1280]{3,2,1,0:T(8,128)S(1)}, f32[8,2,128,1280]{3,2,1,0:T(8,128)}, u32[]{:S(2)}) copy-start(f32[8,2,128,1280]{3,2,1,0:T(8,128)} %get-tuple-element.189) | copy-start | bytes 31457284 | tf_op jit(solution)/shard_map/while
  155.3 4.2 %copy-start.5 = (bf16[256,512]{0,1:T(8,128)(2,1)S(1)}, bf16[256,512]{0,1:T(8,128)(2,1)}, u32[]{:S(2)}) copy-start(bf16[256,512]{0,1:T(8,128)(2,1)} %get-tuple-element.194) | copy-start | bytes 786436 | tf_op jit(solution)/shard_map/while
  179.6 4.0 %copy-start.2 = (bf16[2,128,8,64]{1,0,3,2:T(2,128)(2,1)S(1)}, bf16[2,128,8,64]{1,0,3,2:T(2,128)(2,1)}, u32[]{:S(2)}) copy-start(bf16[2,128,8,64]{1,0,3,2:T(2,128)(2,1)} %reshape.408) | copy-start | bytes 786436 | tf_op jit(solution)/shard_map/while
  183.5 8.1 %copy-start.3 = (bf16[1280,512]{0,1:T(8,128)(2,1)S(1)}, bf16[1280,512]{0,1:T(8,128)(2,1)}, u32[]{:S(2)}) copy-start(bf16[1280,512]{0,1:T(8,128)(2,1)} %get-tuple-element.187) | copy-start | bytes 3932164 | tf_op jit(solution)/shard_map/while
  185.2 7.0 %copy-start.1 = (f32[8,2,128,1280]{3,2,1,0:T(8,128)S(1)}, f32[8,2,128,1280]{3,2,1,0:T(8,128)}, u32[]{:S(2)}) copy-start(f32[8,2,128,1280]{3,2,1,0:T(8,128)} %get-tuple-element.189) | copy-start | bytes 31457284 | tf_op jit(solution)/shard_map/while
  192.1 4.2 %copy-start.5 = (bf16[256,512]{0,1:T(8,128)(2,1)S(1)}, bf16[256,512]{0,1:T(8,128)(2,1)}, u32[]{:S(2)}) copy-start(bf16[256,512]{0,1:T(8,128)(2,1)} %get-tuple-element.194) | copy-start | bytes 786436 | tf_op jit(solution)/shard_map/while
  204.1 1.4 copy-start.6
  204.1 1.7 copy-start.13
